TPU v7x, 32 devices: a whole 2x2x4 slice. The times are simulated.
32 devices in a mesh: env: 4 (over z), tm: 8 (over y, x, core).
Axes of the slice: x: 2, y: 2, z: 4, core: 2. Of those that a mesh axis runs over, the one named last changes fastest.
Arguments:
- observations: bfloat16 [8, 6144, 2048], P('env', 'tm'), may hold values from -6 to 6
- stored_values: float32 [8, 6144], P('env', 'tm'), may hold values from -3.6 to 3.6
- rewards: float32 [8, 6144], P('env', 'tm'), may hold values from -0.18 to 0.18
- episode_ends: int32 [8, 6144], P('env', 'tm'), may hold values 0 or 1
- stale_list: int32 [4, 8, 12], P('env', 'tm'), may hold values from -1 to 11, as said below
- discount_horizon: float32 [8], P('env'), may hold values from 10 to 49152
- trace_horizon: float32 [8], P('env'), may hold values from 10 to 49152
- bootstrap: float32 [8], P('env'), may hold values from -3.6 to 3.6
- norm_gain: float32 [2048], replicated, may hold values from 0.1 to 1.9
- input_weight: bfloat16 [2048, 4096], replicated, may hold values from -0.125 to 0.125
- value_head: bfloat16 [4096], replicated, may hold values from -0.09375 to 0.09375
Outputs:
- targets: float32 [8, 6144], P('env', 'tm')
- advantages: float32 [8, 6144], P('env', 'tm')
Inputs may be any that keep to these rules, and one draw needn't show every extreme that they name: `stale_list`: for each device (first two indices: env shard, time shard) the last dimension lists distinct local block numbers e * 6 + k (e an environment row within the env shard, k a block of 128 steps within the time shard), followed by -1 entries; on some device all 12 blocks are listed.
All inputs are finite; a program needn't handle non-finite values. No bound on the sum of `episode_ends` on one device may be relied on, other than what follows from the above.
Results may differ from a plain program's by a relative error of at most 0.0018.
Values may be sent and summed in bfloat16 or wider, within the bound.
A program may use at most 128 MiB of HBM per device.

v0:
```python
import jax
import jax.numpy as jnp
from jax import lax
from jax.sharding import PartitionSpec as P

BLOCK = 128


blocks_per_turn = 4


def shifted(value, axis, by):
    count = lax.axis_size(axis)
    pairs = [(i, i + by) for i in range(count) if 0 <= i + by < count]
    return lax.ppermute(value, axis, pairs)


def entering(value, axis, combine, identity):
    count, index = (lax.axis_size(axis), lax.axis_index(axis))
    everything = jax.tree.map(lambda part: lax.all_gather(part, axis), value)
    start = jax.tree.map(
        lambda part, zero: jnp.broadcast_to(jnp.asarray(zero, part.dtype), part.shape),
        value,
        identity,
    )

    def turn(k, before):
        at = count - 1 - k
        reached = at > index
        new = combine(before, jax.tree.map(lambda part: part[at], everything))
        return jax.tree.map(lambda a, b: jnp.where(reached, a, b), new, before)

    return lax.fori_loop(0, count, turn, start)


def critic_rows(block_rows, norm_gain, input_weight, value_head):
    widened = block_rows.astype(jnp.float32)
    square_mean = jnp.mean(widened * widened, axis=-1, keepdims=True)
    normed = (widened * lax.rsqrt(square_mean + 1e-05) * norm_gain).astype(jnp.bfloat16)
    hidden = jnp.dot(normed, input_weight, preferred_element_type=jnp.float32)
    active = jax.nn.silu(hidden).astype(jnp.bfloat16)
    return jnp.dot(active, value_head, preferred_element_type=jnp.float32)


def evaluate(blocks, live, norm_gain, input_weight, value_head):
    slot_count, steps, features = blocks.shape
    live_first = jnp.argsort(jnp.where(live, 0, 1).astype(jnp.int32), stable=True)
    live_count = jnp.sum(live.astype(jnp.int32))
    turn_count = (live_count + blocks_per_turn - 1) // blocks_per_turn

    def one_turn(turn_index, scores):
        chosen = lax.dynamic_slice_in_dim(live_first, turn_index * blocks_per_turn, blocks_per_turn)
        gathered = jnp.take(blocks, chosen, axis=0).reshape(blocks_per_turn * steps, features)
        scored = critic_rows(gathered, norm_gain, input_weight, value_head).reshape(
            blocks_per_turn, steps
        )
        return scores.at[chosen].set(scored)

    return lax.fori_loop(0, turn_count, one_turn, jnp.zeros((slot_count, steps), jnp.float32))


def local_sweep(decay_rate, td_error):

    def compose_steps(earlier, later):
        return (later[0] * earlier[0], later[1] + later[0] * earlier[1])

    factor, offset = lax.associative_scan(
        compose_steps, (decay_rate[:, ::-1], td_error[:, ::-1]), axis=1
    )
    return (factor[:, ::-1], offset[:, ::-1])


def compose_pair(earlier, later):
    return (later[0] * earlier[0], later[1] + later[0] * earlier[1])


def on_device(
    observations,
    stored_values,
    rewards,
    episode_ends,
    stale_list,
    discount_horizon,
    trace_horizon,
    bootstrap,
    norm_gain,
    input_weight,
    value_head,
):
    env_rows, local_steps, features = observations.shape
    local_blocks = env_rows * local_steps // BLOCK
    blocks = observations.reshape(local_blocks, BLOCK, features)
    listed = stale_list.reshape(local_blocks)
    numbers = jnp.arange(local_blocks, dtype=jnp.int32)
    stale_flags = jnp.any(listed[:, None] == numbers[None, :], axis=0)
    shards = lax.axis_size("tm")
    refreshed = evaluate(blocks, stale_flags, norm_gain, input_weight, value_head)
    values = jnp.where(
        stale_flags[:, None], refreshed, stored_values.reshape(local_blocks, BLOCK)
    ).reshape(env_rows, local_steps)
    discount = 1.0 - 1.0 / discount_horizon
    trace_rate = 1.0 - 1.0 / trace_horizon
    continuing = 1.0 - episode_ends.astype(jnp.float32)
    decay_rate = discount[:, None] * trace_rate[:, None] * continuing
    is_last = lax.axis_index("tm") == shards - 1
    incoming = shifted(values[:, 0], "tm", -1)
    tail_value = jnp.where(is_last, bootstrap, incoming)
    next_values = jnp.concatenate([values[:, 1:], tail_value[:, None]], axis=1)
    td_error = rewards + discount[:, None] * continuing * next_values - values
    factor, offset = local_sweep(decay_rate, td_error)
    identity_pair = (jnp.ones((env_rows,), jnp.float32), jnp.zeros((env_rows,), jnp.float32))
    carried = entering((factor[:, 0], offset[:, 0]), "tm", compose_pair, identity_pair)
    advantage = offset + factor * carried[1][:, None]
    total_count = float(env_rows * lax.axis_size("env") * local_steps * shards)
    adv_mean = lax.psum(jnp.sum(advantage), ("env", "tm")) / total_count
    centered = advantage - adv_mean
    adv_var = lax.psum(jnp.sum(centered * centered), ("env", "tm")) / total_count
    advantages = (advantage - adv_mean) * lax.rsqrt(adv_var + 1e-05)
    return (advantage + values, advantages)


def solution(mesh):
    in_specs = (
        P("env", "tm", None),
        P("env", "tm"),
        P("env", "tm"),
        P("env", "tm"),
        P("env", "tm", None),
        P("env"),
        P("env"),
        P("env"),
        P(),
        P(),
        P(),
    )
    out_specs = (P("env", "tm"), P("env", "tm"))
    return jax.shard_map(
        on_device, mesh=mesh, in_specs=in_specs, out_specs=out_specs, check_vma=False
    )
```

profile of v0, /device:TPU:0, one launch (start us, length us, event | category | flops | bytes accessed | tf_op | source)
XLA Modules:
  0.0 187.7 jit_solution(13805156912195279909)
XLA Ops:
  0.6 0.7 fusion.6
  1.4 0.6 broadcast_select_fusion.4
  2.7 1.3 sort.17
  4.1 63.3 %while.26 = (s32[]{:T(128)}, f32[12,128]{1,0:T(8,128)S(1)}, s32[]{:T(128)}, s32[12]{0:T(128)S(1)}, bf16[12,128,2048]{2,1,0:T(8,128)(2,1)}, /*index=5*/f32[2048]{...) while((s32[]{:T(128)}, f32[12,128]{1,0:T(8,128)S(1)}, ...), condition=%wide.region_6.7_spmd, body=%wide.region_3.6_spmd.sunk | while | flops 8614053888 | bytes 29480252 | solution.py:59
  4.2 3.5 %gather_fusion = bf16[4,128,2048]{2,1,0:T(8,128)(2,1)S(1)} fusion(bf16[12,128,2048]{2,1,0:T(8,128)(2,1)} %get-tuple-element.394, s32[1024]{0:T(1024)S(1)} %pad_clamp_fusion.2), kind=kCustom, calls=%fused_computation.clone.1 | custom fusion | bytes 4194320 | tf_op jit(solution)/shard_map/while/body/jit(_take)/gather | solution.py:53
  7.8 1.7 bitcast_select_fusion.2
  9.5 0.7 multiply_reduce_fusion.3
  10.2 14.3 %fusion.21 = f32[1,512]{1,0:T(1,128)S(1)} fusion(bf16[4096,1]{0,1:T(2,128)(2,1)S(1)} %reshape.102, bf16[2048,4096]{1,0:T(8,128)(2,1)} %get-tuple-element.396, bf16[512,2048]{1,0:T(8,128)(2,1)} %bitcast_select_fusion.2, f32[2048]{0:T(1024)S(1)} %copy-done.7, f32[512]{0:T(512)S(1)} %rsqrt_bitcast_fusion.2), kind=kOutput, calls=%fused_computation.5.clone.1 | convolution fusion | flops 8608808960 | bytes 18894848 | tf_op jit(solution)/shard_map/while/body/dot_general | solution.py:42
  24.6 0.6 scatter_fusion
  25.3 3.5 %gather_fusion = bf16[4,128,2048]{2,1,0:T(8,128)(2,1)S(1)} fusion(bf16[12,128,2048]{2,1,0:T(8,128)(2,1)} %get-tuple-element.394, s32[1024]{0:T(1024)S(1)} %pad_clamp_fusion.2), kind=kCustom, calls=%fused_computation.clone.1 | custom fusion | bytes 4194320 | tf_op jit(solution)/shard_map/while/body/jit(_take)/gather | solution.py:53
  28.9 1.7 bitcast_select_fusion.2
  30.6 0.7 multiply_reduce_fusion.3
  31.3 14.3 %fusion.21 = f32[1,512]{1,0:T(1,128)S(1)} fusion(bf16[4096,1]{0,1:T(2,128)(2,1)S(1)} %reshape.102, bf16[2048,4096]{1,0:T(8,128)(2,1)} %get-tuple-element.396, bf16[512,2048]{1,0:T(8,128)(2,1)} %bitcast_select_fusion.2, f32[2048]{0:T(1024)S(1)} %copy-done.7, f32[512]{0:T(512)S(1)} %rsqrt_bitcast_fusion.2), kind=kOutput, calls=%fused_computation.5.clone.1 | convolution fusion | flops 8608808960 | bytes 18894848 | tf_op jit(solution)/shard_map/while/body/dot_general | solution.py:42
  45.7 0.6 scatter_fusion
  46.4 3.5 %gather_fusion = bf16[4,128,2048]{2,1,0:T(8,128)(2,1)S(1)} fusion(bf16[12,128,2048]{2,1,0:T(8,128)(2,1)} %get-tuple-element.394, s32[1024]{0:T(1024)S(1)} %pad_clamp_fusion.2), kind=kCustom, calls=%fused_computation.clone.1 | custom fusion | bytes 4194320 | tf_op jit(solution)/shard_map/while/body/jit(_take)/gather | solution.py:53
  50.0 1.7 bitcast_select_fusion.2
  51.7 0.7 multiply_reduce_fusion.3
  52.5 14.3 %fusion.21 = f32[1,512]{1,0:T(1,128)S(1)} fusion(bf16[4096,1]{0,1:T(2,128)(2,1)S(1)} %reshape.102, bf16[2048,4096]{1,0:T(8,128)(2,1)} %get-tuple-element.396, bf16[512,2048]{1,0:T(8,128)(2,1)} %bitcast_select_fusion.2, f32[2048]{0:T(1024)S(1)} %copy-done.7, f32[512]{0:T(512)S(1)} %rsqrt_bitcast_fusion.2), kind=kOutput, calls=%fused_computation.5.clone.1 | convolution fusion | flops 8608808960 | bytes 18894848 | tf_op jit(solution)/shard_map/while/body/dot_general | solution.py:42
  66.8 0.6 scatter_fusion
  67.6 1.5 collective-permute-start
  69.2 0.7 dynamic-slice
  70.9 0.2 slice.307
  71.1 0.2 slice.311
  71.3 0.2 slice.309
  71.6 0.2 slice.315
  71.8 0.3 slice.308
  72.1 0.3 slice.310
  72.4 0.3 slice.312
  72.6 0.3 slice.316
  72.9 0.2 slice.318
  73.1 0.2 slice.320
  73.4 0.2 slice.319
  73.6 0.2 slice.323
  73.8 0.2 slice.325
  74.0 0.2 slice.327
  74.2 0.2 slice.326
  74.4 0.2 slice.330
  78.0 0.2 slice.322
  78.2 0.2 slice.324
  78.4 0.2 slice.314
  78.6 0.2 slice.317
  78.8 0.2 slice.305
  79.1 0.2 slice.303
  79.4 0.3 reverse.11
  84.1 0.2 pad.142
  84.3 0.2 pad.143
  84.6 0.2 pad.145
  84.9 0.2 pad.144
  85.4 0.3 reverse.10
  85.7 0.2 pad.124
  86.0 0.2 pad.125
  86.2 0.2 pad.127
  86.6 0.2 pad.126
  87.0 0.2 dynamic-update-slice.1
  87.3 0.2 dynamic-update-slice
  87.5 12.8 %all-reduce.38 = (f32[16]{0:T(128)S(1)}, f32[16]{0:T(128)S(1)}) all-reduce(f32[16]{0:T(128)S(1)} %dynamic-update-slice, f32[16]{0:T(128)S(1)} %dynamic-update-slice.1), channel_id=2, replica_groups=mesh['env'=4,'tm'=8] {'tm'}, use_global_device_ids=true, to_apply=%add.36 | all-reduce | flops 32 | bytes 256
  100.5 0.4 while.27
  100.8 0.5 rev.9
  101.4 0.5 rev.8
  101.9 0.7 fusion.13
  102.6 43.0 %psum.14 = f32[]{:T(128)} all-reduce(f32[]{:T(128)} %get-tuple-element.229), channel_id=1, replica_groups=mesh['env'=4,'tm'=8] {'env','tm'}, use_global_device_ids=true, to_apply=%region_10.11 | all-reduce | flops 1 | bytes 8 | tf_op jit(solution)/shard_map/psum | solution.py:115
  146.2 0.6 multiply_reduce_fusion.1
  146.8 39.6 %psum.15 = f32[]{:T(128)} all-reduce(f32[]{:T(128)} %multiply_reduce_fusion.1), channel_id=1, replica_groups=mesh['env'=4,'tm'=8] {'env','tm'}, use_global_device_ids=true, to_apply=%region_12.13 | all-reduce | flops 1 | bytes 8 | tf_op jit(solution)/shard_map/psum | solution.py:117
  187.0 0.6 subtract_multiply_fusion
  (183 shorter events, 9.9 us)
Async XLA Ops:
  4.0 63.4 %copy-start.1 = (f32[2,768]{1,0:T(2,128)S(1)}, f32[2,768]{1,0:T(2,128)}, u32[]{:S(2)}) copy-start(f32[2,768]{1,0:T(2,128)} %param.16) | copy-start | bytes 18436
  4.0 65.2 %copy-start.4 = (f32[2]{0:T(128)S(1)}, f32[2]{0:T(128)}, u32[]{:S(2)}) copy-start(f32[2]{0:T(128)} %param.21) | copy-start | bytes 28
  4.0 65.2 %copy-start.5 = (f32[2]{0:T(128)S(1)}, f32[2]{0:T(128)}, u32[]{:S(2)}) copy-start(f32[2]{0:T(128)} %param.20) | copy-start | bytes 28
  4.0 65.2 %copy-start.8 = (u32[32]{0:T(128)S(1)}, u32[32]{0:T(128)}, u32[]{:S(2)}) copy-start(u32[32]{0:T(128)} %constant.199) | copy-start | bytes 388
  4.0 66.7 %copy-start.6 = (f32[2]{0:T(128)S(1)}, f32[2]{0:T(128)}, u32[]{:S(2)}) copy-start(f32[2]{0:T(128)} %param.22) | copy-start | bytes 28
  4.1 66.7 %copy-start.2 = (s32[2,768]{1,0:T(2,128)S(1)}, s32[2,768]{1,0:T(2,128)}, u32[]{:S(2)}) copy-start(s32[2,768]{1,0:T(2,128)} %param.18) | copy-start | bytes 18436
  4.1 66.7 %copy-start.3 = (f32[2,768]{1,0:T(2,128)S(1)}, f32[2,768]{1,0:T(2,128)}, u32[]{:S(2)}) copy-start(f32[2,768]{1,0:T(2,128)} %param.17) | copy-start | bytes 18436
  7.7 2.5 %copy-start = (bf16[4096]{0:T(1024)(128)(2,1)S(1)}, bf16[4096]{0:T(1024)(128)(2,1)}, u32[]{:S(2)}) copy-start(bf16[4096]{0:T(1024)(128)(2,1)} %get-tuple-element.397) | copy-start | bytes 24580 | tf_op jit(solution)/shard_map/while
  7.7 2.5 %copy-start.7 = (f32[2048]{0:T(1024)S(1)}, f32[2048]{0:T(1024)}, u32[]{:S(2)}) copy-start(f32[2048]{0:T(1024)} %get-tuple-element.395) | copy-start | bytes 24580 | tf_op jit(solution)/shard_map/while
  28.8 2.5 %copy-start = (bf16[4096]{0:T(1024)(128)(2,1)S(1)}, bf16[4096]{0:T(1024)(128)(2,1)}, u32[]{:S(2)}) copy-start(bf16[4096]{0:T(1024)(128)(2,1)} %get-tuple-element.397) | copy-start | bytes 24580 | tf_op jit(solution)/shard_map/while
  28.8 2.5 %copy-start.7 = (f32[2048]{0:T(1024)S(1)}, f32[2048]{0:T(1024)}, u32[]{:S(2)}) copy-start(f32[2048]{0:T(1024)} %get-tuple-element.395) | copy-start | bytes 24580 | tf_op jit(solution)/shard_map/while
  49.9 2.5 %copy-start = (bf16[4096]{0:T(1024)(128)(2,1)S(1)}, bf16[4096]{0:T(1024)(128)(2,1)}, u32[]{:S(2)}) copy-start(bf16[4096]{0:T(1024)(128)(2,1)} %get-tuple-element.397) | copy-start | bytes 24580 | tf_op jit(solution)/shard_map/while
  49.9 2.5 %copy-start.7 = (f32[2048]{0:T(1024)S(1)}, f32[2048]{0:T(1024)}, u32[]{:S(2)}) copy-start(f32[2048]{0:T(1024)} %get-tuple-element.395) | copy-start | bytes 24580 | tf_op jit(solution)/shard_map/while
  67.6 3.0 %collective-permute-start = (f32[2]{0:T(128)S(1)}, f32[2]{0:T(128)S(1)}, u32[]{:S(2)}, u32[]{:S(2)}) collective-permute-start(f32[2]{0:T(128)S(1)} %slice_reduce_fusion), channel_id=1, source_target_pairs={{1,0},{2,1},{3,2},{4,3},{5,4},{6,5},{7,6},{9,8},{10,9},{11,10},{12... | collective-permute-start | bytes 32 | tf_op jit(solution)/shard_map/ppermute | solution.py:15
where the time goes:
time: 188 us
  blocking collectives  95.4 us (51%)
  matrix products  43 us (23%)
  local copies, waits for them, and re-layouts  28.8 us (15%)
  other arithmetic  14.7 us (8%)
  between operations  3.81 us (2%)
    dot_general x3, matrix products, critic_rows(): return jnp.dot(active, value_head, preferred_element_type=jnp.float32)  43 us
    psum x1, blocking collectives, on_device(): adv_mean = lax.psum(jnp.sum(advantage), ('env', 'tm')) / total_count  43 us
    psum x1, blocking collectives, on_device(): lax.psum(jnp.sum(centered * centered), ('env', 'tm')) / total_count  39.6 us
    unnamed x1, blocking collectives  12.8 us
    gather x3, local copies, waits for them, and re-layouts, one_turn(): jnp.take(blocks, chosen, axis=0).reshape(blocks_per_turn * steps, features)  10.4 us
    slice x58, local copies, waits for them, and re-layouts, local_sweep(): lax.associative_scan(compose_steps, (decay_rate[:, ::-1], td_error[:, ::-...  8.38 us
    select_n x3, other arithmetic, one_turn(): jnp.take(blocks, chosen, axis=0).reshape(blocks_per_turn * steps, features)  5.2 us
    pad x34, local copies, waits for them, and re-layouts, local_sweep(): lax.associative_scan(compose_steps, (decay_rate[:, ::-1], td_error[:, ::-...  4.63 us
  transfers between devices with their start and end apart: 1, of which 1 were waited for; matrix products, arithmetic and copies ran while one was open for 0% of the time, Pallas kernels for 0%

commit v1 on v0

v1 whole, which is shorter than its diff:
```python
import functools

import jax
import jax.numpy as jnp
from jax import lax
from jax.experimental import pallas as pl
from jax.experimental.pallas import tpu as pltpu
from jax.sharding import PartitionSpec as P

BLOCK = 128
CHUNK = 256
MESH = pl.DeviceIdType.MESH


def critic_kernel(
    list_ref, blocks_ref, weight_ref, stored_ref, gain_ref, head_ref, out_ref,
    rows_ref, w_ref, acc_ref, row_sems, w_sems,
):
    slots, steps, features = blocks_ref.shape
    env_rows = stored_ref.shape[0]
    per_env = slots // env_rows
    chunks = w_ref.shape[0]
    count = jnp.int32(0)
    for i in range(slots):
        count = count + jnp.where(list_ref[i] >= 0, 1, 0).astype(jnp.int32)

    def row_copy(i):
        number = jnp.maximum(list_ref[i], 0)
        return pltpu.make_async_copy(
            blocks_ref.at[number], rows_ref.at[pl.ds(i * steps, steps)], row_sems.at[i]
        )

    def weight_copy(c):
        return pltpu.make_async_copy(
            weight_ref.at[:, pl.ds(pl.multiple_of(c * CHUNK, CHUNK), CHUNK)], w_ref.at[c], w_sems.at[c]
        )

    for k in range(per_env):
        out_ref[k * env_rows:(k + 1) * env_rows, :] = stored_ref[:, k * steps:(k + 1) * steps]

    @pl.when(count > 0)
    def _():
        @pl.loop(0, count)
        def _(i):
            row_copy(i).start()

        @pl.loop(0, chunks)
        def _(c):
            weight_copy(c).start()

        acc_ref[...] = jnp.zeros_like(acc_ref)

        @pl.loop(0, count)
        def _(i):
            row_copy(i).wait()
            here = pl.ds(pl.multiple_of(i * steps, steps), steps)
            wide = rows_ref[here, :].astype(jnp.float32)
            mean = jnp.sum(wide * wide, axis=-1, keepdims=True) * (1.0 / features)
            rows_ref[here, :] = (wide * lax.rsqrt(mean + 1e-05) * gain_ref[...]).astype(jnp.bfloat16)

        def tile(c, start, size):
            here = pl.ds(pl.multiple_of(start, steps), size)
            hidden = jnp.dot(rows_ref[here, :], w_ref[c], preferred_element_type=jnp.float32)
            half = 0.5 * hidden
            active = (half + half * jnp.tanh(half)).astype(jnp.bfloat16).astype(jnp.float32)
            part = active * head_ref[c]
            total = part[:, :128]
            for j in range(1, CHUNK // 128):
                total = total + part[:, j * 128:(j + 1) * 128]
            acc_ref[here, :] += total

        @pl.loop(0, chunks)
        def _(c):
            weight_copy(c).wait()

            @pl.loop(0, count // 4)
            def _(q):
                tile(c, q * (4 * steps), 4 * steps)

            @pl.when(count % 4 >= 2)
            def _():
                tile(c, (count // 4) * (4 * steps), 2 * steps)

            @pl.when(count % 2 == 1)
            def _():
                tile(c, (count - 1) * steps, steps)

        @pl.loop(0, count)
        def _(i):
            here = pl.ds(pl.multiple_of(i * steps, steps), steps)
            score = jnp.sum(acc_ref[here, :].T, axis=0, keepdims=True)
            number = list_ref[i]
            out_ref[pl.ds((number % per_env) * env_rows + number // per_env, 1), :] = score


def critic_values(listed, blocks, weight, stored, gain, head):
    slots, steps, features = blocks.shape
    hidden = weight.shape[1]
    chunks = hidden // CHUNK
    vmem = pl.BlockSpec(memory_space=pltpu.VMEM)
    hbm = pl.BlockSpec(memory_space=pl.ANY)
    return pl.pallas_call(
        critic_kernel,
        out_shape=jax.ShapeDtypeStruct((slots, steps), jnp.float32),
        in_specs=[pl.BlockSpec(memory_space=pltpu.SMEM), hbm, hbm, vmem, vmem, vmem],
        out_specs=vmem,
        scratch_shapes=[
            pltpu.VMEM((slots * steps, features), jnp.bfloat16),
            pltpu.VMEM((chunks, features, CHUNK), jnp.bfloat16),
            pltpu.VMEM((slots * steps, 128), jnp.float32),
            pltpu.SemaphoreType.DMA((slots,)),
            pltpu.SemaphoreType.DMA((chunks,)),
        ],
        compiler_params=pltpu.CompilerParams(vmem_limit_bytes=60 * 1024 * 1024),
        name="critic",
    )(listed, blocks, weight, stored, gain, head)


def sweep_kernel(
    n_env, n_tm, dh_ref, th_ref, boot_ref, values_ref, rewards_ref, ends_ref, targets_ref, adv_ref,
    tm_buf, env_buf, tm_send, tm_recv, env_send, env_recv,
):
    env_rows, local_steps = rewards_ref.shape
    rows, steps = values_ref.shape
    per_env = rows // env_rows
    my_env, my_tm = lax.axis_index("env"), lax.axis_index("tm")

    barrier = pltpu.get_barrier_semaphore()
    for d in range(1, n_tm):
        pl.semaphore_signal(barrier, inc=1, device_id=(my_env, lax.rem(my_tm + d, n_tm)), device_id_type=MESH)
    for d in range(1, n_env):
        pl.semaphore_signal(barrier, inc=1, device_id=(lax.rem(my_env + d, n_env), my_tm), device_id_type=MESH)

    def stacked(ref):
        return jnp.concatenate([ref[:, k * steps:(k + 1) * steps] for k in range(per_env)], axis=0)

    def by_env(ref, shape, modulus):
        env_of = lax.broadcasted_iota(jnp.int32, shape, 0) % modulus
        out = jnp.full(shape, ref[0], jnp.float32)
        for e in range(1, env_rows):
            out = jnp.where(env_of == e, ref[e], out)
        return out

    def over_blocks(x):
        total = x[:env_rows]
        for k in range(1, per_env):
            total = total + x[k * env_rows:(k + 1) * env_rows]
        return total

    def mean_of(x):
        total = jnp.sum(over_blocks(x), axis=1, keepdims=True) * (1.0 / local_steps)
        return jnp.broadcast_to(total, (env_rows, steps))

    full = (rows, steps)
    lane = lax.broadcasted_iota(jnp.int32, full, 1)
    row = lax.broadcasted_iota(jnp.int32, full, 0)
    values = values_ref[...]
    rewards = stacked(rewards_ref)
    going = 1.0 - stacked(ends_ref).astype(jnp.float32)
    discount = 1.0 - 1.0 / by_env(dh_ref, full, env_rows)
    trace_rate = 1.0 - 1.0 / by_env(th_ref, full, env_rows)
    reach = discount * going
    decay = discount * trace_rate * going

    last = jnp.logical_and(lane == steps - 1, row >= rows - env_rows)
    head_of_row = jnp.broadcast_to(values[:, :1], full)
    after_row = jnp.concatenate([head_of_row[env_rows:], jnp.zeros((env_rows, steps), jnp.float32)], axis=0)
    following = jnp.where(lane == steps - 1, after_row, pltpu.roll(values, steps - 1, 1))
    offset = rewards + reach * following - values
    factor = jnp.where(last, 1.0, decay)

    by = 1
    while by < steps:
        inside = lane < steps - by
        f_next = jnp.where(inside, pltpu.roll(factor, steps - by, 1), 1.0)
        o_next = jnp.where(inside, pltpu.roll(offset, steps - by, 1), 0.0)
        offset = offset + factor * o_next
        factor = factor * f_next
        by *= 2
    f_row = jnp.broadcast_to(factor[:, :1], full)
    o_row = jnp.broadcast_to(offset[:, :1], full)
    f_tail = [jnp.ones((env_rows, steps), jnp.float32)]
    o_tail = [jnp.zeros((env_rows, steps), jnp.float32)]
    for k in range(per_env - 1, 0, -1):
        f_here = f_row[k * env_rows:(k + 1) * env_rows]
        o_here = o_row[k * env_rows:(k + 1) * env_rows]
        o_tail.insert(0, o_here + f_here * o_tail[0])
        f_tail.insert(0, f_here * f_tail[0])
    offset = offset + factor * jnp.concatenate(o_tail, axis=0)
    factor = factor * jnp.concatenate(f_tail, axis=0)

    o_mean, f_mean = mean_of(offset), mean_of(factor)
    o_dev = offset - jnp.concatenate([o_mean] * per_env, axis=0)
    f_dev = factor - jnp.concatenate([f_mean] * per_env, axis=0)
    small = (env_rows, steps)

    def spread(x, at):
        return jnp.broadcast_to(x[:, at:at + 1], small)

    parts = [
        spread(factor[:env_rows], 0),
        spread(offset[:env_rows], 0),
        spread(values[:env_rows], 0),
        spread(reach[rows - env_rows:], steps - 1),
        spread(decay[rows - env_rows:], steps - 1),
        o_mean, f_mean, mean_of(o_dev * o_dev), mean_of(o_dev * f_dev), mean_of(f_dev * f_dev),
    ]
    small_lane = lax.broadcasted_iota(jnp.int32, small, 1)
    message = jnp.zeros(small, jnp.float32)
    for q, part in enumerate(parts):
        message = jnp.where(small_lane == q, part, message)
    tm_buf[0] = message

    pl.semaphore_wait(barrier, n_tm - 1 + n_env - 1)
    copies = [
        pltpu.make_async_remote_copy(
            src_ref=tm_buf.at[0], dst_ref=tm_buf.at[d], send_sem=tm_send.at[d], recv_sem=tm_recv.at[d],
            device_id=(my_env, lax.rem(my_tm + d, n_tm)), device_id_type=MESH,
        )
        for d in range(1, n_tm)
    ]
    for copy in copies:
        copy.start()
    for copy in copies:
        copy.wait()

    next_value = by_env(boot_ref, small, env_rows)
    next_adv = jnp.zeros(small, jnp.float32)
    my_entry = jnp.zeros(small, jnp.float32)
    means, spreads = [], []
    for k in range(n_tm - 1, -1, -1):
        got = tm_buf[lax.rem(my_tm + n_tm - k, n_tm)]
        f0, o0, v0, reach_l, decay_l, om, fm, oo, of, ff = [spread(got, q) for q in range(len(parts))]
        entry = reach_l * next_value + decay_l * next_adv
        my_entry = jnp.where(k == my_tm, entry, my_entry)
        means.append(om + fm * entry)
        spreads.append(oo + (2.0 * of + ff * entry) * entry)
        next_adv = o0 + f0 * entry
        next_value = v0

    def row_mean(x):
        return jnp.broadcast_to(jnp.sum(x, axis=0, keepdims=True) * (1.0 / env_rows), small)

    group_mean = row_mean(sum(means)) * (1.0 / n_tm)
    group_var = row_mean(sum(s + (m - group_mean) * (m - group_mean) for m, s in zip(means, spreads))) * (1.0 / n_tm)
    env_buf[0] = jnp.where(small_lane == 0, group_mean, group_var)
    copies = [
        pltpu.make_async_remote_copy(
            src_ref=env_buf.at[0], dst_ref=env_buf.at[d], send_sem=env_send.at[d], recv_sem=env_recv.at[d],
            device_id=(lax.rem(my_env + d, n_env), my_tm), device_id_type=MESH,
        )
        for d in range(1, n_env)
    ]
    for copy in copies:
        copy.start()
    advantage = offset + factor * jnp.concatenate([my_entry] * per_env, axis=0)
    targets = advantage + values
    for k in range(per_env):
        targets_ref[:, k * steps:(k + 1) * steps] = targets[k * env_rows:(k + 1) * env_rows]
    for copy in copies:
        copy.wait()
    got = [env_buf[lax.rem(my_env + n_env - j, n_env)] for j in range(n_env)]
    env_means = [spread(g, 0) for g in got]
    mean = sum(env_means) * (1.0 / n_env)
    var = sum(spread(g, 1) + (m - mean) * (m - mean) for g, m in zip(got, env_means)) * (1.0 / n_env)
    scale = lax.rsqrt(var + 1e-05)
    for k in range(per_env):
        adv_ref[:, k * steps:(k + 1) * steps] = (advantage[k * env_rows:(k + 1) * env_rows] - mean) * scale


def sweep(n_env, n_tm, dh, th, boot, values, rewards, ends):
    env_rows, local_steps = rewards.shape
    vmem = pl.BlockSpec(memory_space=pltpu.VMEM)
    smem = pl.BlockSpec(memory_space=pltpu.SMEM)
    return pl.pallas_call(
        functools.partial(sweep_kernel, n_env, n_tm),
        out_shape=[jax.ShapeDtypeStruct((env_rows, local_steps), jnp.float32)] * 2,
        in_specs=[smem] * 3 + [vmem] * 3,
        out_specs=[vmem] * 2,
        scratch_shapes=[
            pltpu.VMEM((n_tm, env_rows, BLOCK), jnp.float32),
            pltpu.VMEM((n_env, env_rows, BLOCK), jnp.float32),
            pltpu.SemaphoreType.DMA((n_tm,)),
            pltpu.SemaphoreType.DMA((n_tm,)),
            pltpu.SemaphoreType.DMA((n_env,)),
            pltpu.SemaphoreType.DMA((n_env,)),
        ],
        compiler_params=pltpu.CompilerParams(collective_id=0, has_side_effects=True),
        name="sweep",
    )(dh, th, boot, values, rewards, ends)


def on_device(
    n_env, n_tm, observations, stored_values, rewards, episode_ends, stale_list,
    discount_horizon, trace_horizon, bootstrap, norm_gain, input_weight, value_head,
):
    env_rows, local_steps, features = observations.shape
    slots = env_rows * local_steps // BLOCK
    blocks = observations.reshape(slots, BLOCK, features)
    hidden = input_weight.shape[1]
    values = critic_values(
        stale_list.reshape(slots), blocks, input_weight, stored_values, norm_gain.reshape(1, features),
        value_head.astype(jnp.float32).reshape(hidden // CHUNK, 1, CHUNK),
    )
    return tuple(sweep(
        n_env, n_tm, discount_horizon, trace_horizon, bootstrap, values, rewards, episode_ends
    ))


def solution(mesh):
    in_specs = (
        P("env", "tm", None), P("env", "tm"), P("env", "tm"), P("env", "tm"), P("env", "tm", None),
        P("env"), P("env"), P("env"), P(), P(), P(),
    )
    return jax.shard_map(
        functools.partial(on_device, mesh.shape["env"], mesh.shape["tm"]),
        mesh=mesh, in_specs=in_specs, out_specs=(P("env", "tm"), P("env", "tm")), check_vma=False,
    )
```

time: 188 us -> 60.3 us (0.32)
  blocking collectives: 95.4 us -> 0 us
  Pallas kernels: 0 us -> 55.2 us
  matrix products: 43 us -> 0 us
  local copies, waits for them, and re-layouts: 28.8 us -> 2.57 us
  other arithmetic: 14.7 us -> 1.3 us
  between operations: 3.81 us -> 0.65 us
    psum x2 -> x0, blocking collectives: 82.5 us -> none  [the longest x1 43 us: on_device(): adv_mean = lax.psum(jnp.sum(advantage), ('env', 'tm')) / total_count]
    pallas_call x0 -> x2, Pallas kernels: none -> 55.2 us  [the longest x1 38.7 us: sweep(): pl.pallas_call(functools.partial(sweep_kernel, n_env, n_tm), out_shape=[j...]
    dot_general x3 -> x0, matrix products: 43 us -> none  [critic_rows(): return jnp.dot(active, value_head, preferred_element_type=jnp.float32)]
    unnamed x1 -> x0, blocking collectives: 12.8 us -> none
    gather x3 -> x0, local copies, waits for them, and re-layouts: 10.4 us -> none  [one_turn(): jnp.take(blocks, chosen, axis=0).reshape(blocks_per_turn * steps, features)]
    slice x60 -> x0, local copies, waits for them, and re-layouts: 8.57 us -> none  [the longest x58 8.38 us: local_sweep(): lax.associative_scan(compose_steps, (decay_rate[:, ::-1], td_error[:, ::-...]
    select_n x13 -> x0, other arithmetic: 6.05 us -> none  [the longest x3 5.2 us: one_turn(): jnp.take(blocks, chosen, axis=0).reshape(blocks_per_turn * steps, features)]
    pad x34 -> x0, local copies, waits for them, and re-layouts: 4.63 us -> none  [local_sweep(): lax.associative_scan(compose_steps, (decay_rate[:, ::-1], td_error[:, ::-...]
  transfers between devices with their start and end apart: 1 -> 0, of which waited for: 1 -> 0; matrix products, arithmetic and copies ran while one was open for 0% -> 0% of each run, Pallas kernels for 0% -> 0%
where the time goes in v1:
time: 60.3 us; the launch traced here: 59.8 us
  Pallas kernels  55.2 us (92%)
  local copies, waits for them, and re-layouts  2.57 us (4%)
  other arithmetic  1.3 us (2%)
  between operations  0.65 us (1%)
    pallas_call x1, Pallas kernels, sweep(): pl.pallas_call(functools.partial(sweep_kernel, n_env, n_tm), out_shape=[j...  38.7 us
    pallas_call x1, Pallas kernels, critic_values(): pl.pallas_call(critic_kernel, out_shape=jax.ShapeDtypeStruct((slots, step...  16.5 us
    unnamed x2, local copies, waits for them, and re-layouts  2.57 us
    reshape x1, other arithmetic, on_device(): value_head.astype(jnp.float32).reshape(hidden // CHUNK, 1, CHUNK)  1.3 us

profile of v1, /device:TPU:0, one launch (start us, length us, event | category | flops | bytes accessed | tf_op | source)
XLA Modules:
  0.0 59.8 jit_solution(10127025300042350115)
XLA Ops:
  0.6 1.3 %reshape.23 = f32[4096]{0:T(1024)} convert(bf16[4096]{0:T(1024)(128)(2,1)} %param.21) | non-fusion elementwise | flops 4096 | bytes 24576 | tf_op jit(solution)/shard_map/reshape | solution.py:303
  1.9 16.5 %critic.1.values_ref = f32[12,128]{1,0:T(8,128)} custom-call(s32[12]{0:T(128)} %bitcast.7, bf16[12,128,2048]{2,1,0:T(8,128)(2,1)} %bitcast.4, bf16[2048,4096]{1,0:T(8,128)(2,1)} %weight_ref.1, f32[2,768]{1,0:T(2,128)} %stored_ref.1, f32[1,2048]{1,0:T(1,128)} %bitcast.6, f32[16,1,256]{2,1,0:T(1,128)} %bitcast.5), custom_call_target="tpu_custom_call" | custom-call | tf_op jit(solution)/shard_map/critic/pallas_call | solution.py:102
  18.4 38.7 %sweep.1 = (f32[2,768]{1,0:T(2,128)}, f32[2,768]{1,0:T(2,128)}) custom-call(f32[2]{0:T(128)} %dh_ref.1, f32[2]{0:T(128)} %th_ref.1, f32[2]{0:T(128)} %boot_ref.1, f32[12,128]{1,0:T(8,128)} %critic.1.values_ref, f32[2,768]{1,0:T(2,128)} %rewards_ref.1, s32[2,768]{1,0:T(2,128)} %ends_ref.1), custom_call_target="tpu_custom_call" | custom-call | tf_op jit(solution)/shard_map/sweep/pallas_call | solution.py:275
  57.2 1.3 %copy.15 = f32[2,768]{1,0:T(2,128)} copy(f32[2,768]{1,0:T(2,128)} %get-tuple-element.4) | data formatting | bytes 12288
  58.5 1.3 %copy.16 = f32[2,768]{1,0:T(2,128)} copy(f32[2,768]{1,0:T(2,128)} %get-tuple-element.5) | data formatting | bytes 12288
